TPU v7x, 256 devices: a whole 4x4x8 slice. The times are simulated.
256 devices in a mesh: row: 16 (over x, y), col: 16 (over z, core).
Axes of the slice: x: 4, y: 4, z: 8, core: 2. Of those that a mesh axis runs over, the one named last changes fastest.
Arguments:
- right_side: bfloat16 [16, 16, 8, 128, 256], P('row', 'col'), may hold values from -6 to 6
- diag_inverse: bfloat16 [16, 16, 8, 128, 128], P('row', 'col'), may hold values from -0.5 to 0.5
- panels: bfloat16 [7, 16, 800, 128, 128], P(None, 'row', 'col'), may hold values from -0.0546875 to 0.0546875
- tile_source: int32 [7, 16, 800], P(None, 'row', 'col'), may hold values from 0 to 15
- tile_target: int32 [7, 16, 800], P(None, 'row', 'col'), may hold values from 0 to 15
Outputs:
- solution: float32 [16, 16, 8, 128, 256], P('row', 'col')
All inputs are finite; a program needn't handle non-finite values.
Results may differ from a plain program's by a relative error of at most 0.017.
Values may be sent and summed in bfloat16 or wider, within the bound.
A program may use at most 128 MiB of HBM per device.

v0:
```python
import jax
import jax.numpy as jnp
from jax import lax
from jax.sharding import PartitionSpec as P


def joined_along(parts, dim):
    parts = jnp.moveaxis(parts, 0, dim)
    lengths = parts.shape
    return parts.reshape(*lengths[:dim], lengths[dim] * lengths[dim + 1], *lengths[dim + 2 :])


def sent_to_all(x, axis):
    copies = jnp.broadcast_to(x, (lax.axis_size(axis), *x.shape))
    return lax.all_to_all(copies, axis, split_axis=0, concat_axis=0, tiled=True)


def gather_directly(x, axis, dim):
    return joined_along(sent_to_all(x, axis), dim)


def cut_along(x, dim, size):
    before, after = (x.shape[:dim], x.shape[dim + 1 :])
    return jnp.moveaxis(x.reshape(*before, size, -1, *after), dim, 0)


def sent_and_summed(x, axis, dim):
    parts = cut_along(x, dim, lax.axis_size(axis))
    arrived = lax.all_to_all(parts, axis, split_axis=0, concat_axis=0, tiled=True)
    return arrived.astype(jnp.float32).sum(axis=0)


def local_update(segment, panel, source, target):
    columns = lax.axis_size("col")
    picked = jnp.take(segment, source, axis=0)
    prods = jnp.einsum("qab,qbc->qac", panel, picked, preferred_element_type=jnp.float32)
    onehot = (target[None, :] == jnp.arange(columns, dtype=jnp.int32)[:, None]).astype(jnp.float32)
    sums = jnp.dot(onehot, prods.reshape(prods.shape[0], -1))
    return sums.reshape(columns, prods.shape[1], prods.shape[2]).astype(jnp.bfloat16)


def advance_whole(block, panel, source, target):
    segment = gather_directly(block.astype(jnp.bfloat16)[None], "row", 0)
    partial_value = local_update(segment, panel, source, target)
    return sent_and_summed(partial_value, "col", 0)[0]


def local(right_side, diag_inverse, panels, tile_source, tile_target):
    sections = right_side.shape[2]
    width = right_side.shape[4]
    bounds = [(0, width)]
    incoming = [None for bound in bounds]
    solved = []
    for section in range(sections):
        lower, upper = bounds[0]
        current = right_side[0, 0, section, :, lower:upper].astype(jnp.float32)
        if section > 0:
            current = current - incoming[0]
        block = jnp.dot(
            diag_inverse[0, 0, section],
            current.astype(jnp.bfloat16),
            preferred_element_type=jnp.float32,
        )
        if section + 1 < sections:
            incoming[0] = advance_whole(
                block, panels[section, 0], tile_source[section, 0], tile_target[section, 0]
            )
        solved.append(block)
    return jnp.stack(solved, axis=0)[None, None]


def solution(mesh):
    return jax.shard_map(
        local,
        mesh=mesh,
        in_specs=(
            P("row", "col", None, None, None),
            P("row", "col", None, None, None),
            P(None, "row", "col", None, None),
            P(None, "row", "col"),
            P(None, "row", "col"),
        ),
        out_specs=P("row", "col", None, None, None),
        check_vma=False,
    )
```

profile of v0, /device:TPU:1, one launch (start us, length us, event | category | flops | bytes accessed | tf_op | source)
XLA Modules:
  0.0 508.3 jit_solution(16336328714234556437)
XLA Ops:
  2.8 7.6 %all-to-all-start = ((bf16[16,1,128,256]{3,2,1,0:T(8,128)(2,1)}), bf16[16,1,128,256]{3,2,1,0:T(8,128)(2,1)S(1)}, u32[]{:S(2)}, u32[]{:S(2)}) async-start(bf16[16,1,128,256]{3,2,1,0:T(8,128)(2,1)} %broadcast_in_dim.25), calls=%async_computation | async-start | bytes 2097152 | tf_op jit(solution)/shard_map/all_to_all | solution.py:15
  11.6 14.4 %all-to-all-done = bf16[16,1,128,256]{3,2,1,0:T(8,128)(2,1)S(1)} async-done(((bf16[16,1,128,256]{3,2,1,0:T(8,128)(2,1)}), bf16[16,1,128,256]{3,2,1,0:T(8,128)(2,1)S(1)}, u32[]{:S(2)}, u32[]{:S(2)}) %all-to-all-start) | async-done | bytes 1048608 | tf_op jit(solution)/shard_map/all_to_all | solution.py:15
  28.5 5.3 %fusion.35 = bf16[50,128,256]{1,2,0:T(8,128)(2,1)} fusion(bf16[50,128,256]{2,1,0:T(8,128)(2,1)} %gather_fusion, pred[50]{0:T(512)(128)(4,1)S(1)} %get-tuple-element.35, bf16[7,1,50,128,128]{4,3,2,1,0:T(8,128)(2,1)} %param.9), kind=kOutput, calls=%fused_computation.49 | convolution fusion | flops 421068800 | bytes 8192050 | tf_op jit(solution)/shard_map/qab,qbc->qac/dot_general | solution.py:36
  33.9 4.0 copy.42
  40.7 39.8 %all_to_all.70 = bf16[16,1,128,256]{3,2,1,0:T(8,128)(2,1)S(1)} all-to-all(bf16[16,1,128,256]{3,2,1,0:T(8,128)(2,1)S(1)} %copy.44), channel_id=1, replica_groups=mesh['row'=16,'col'=16] {'col'}, dimensions={0} | all-to-all | bytes 2097152 | tf_op jit(solution)/shard_map/all_to_all | solution.py:29
  87.0 17.3 %all-to-all-done.2 = bf16[16,1,128,256]{3,2,1,0:T(8,128)(2,1)S(1)} async-done(((bf16[16,1,128,256]{3,2,1,0:T(8,128)(2,1)}), bf16[16,1,128,256]{3,2,1,0:T(8,128)(2,1)S(1)}, u32[]{:S(2)}, u32[]{:S(2)}) %all-to-all-start.2) | async-done | bytes 1048608 | tf_op jit(solution)/shard_map/all_to_all | solution.py:15
  106.8 5.3 %fusion.38 = bf16[50,128,256]{1,2,0:T(8,128)(2,1)} fusion(bf16[50,128,256]{2,1,0:T(8,128)(2,1)} %gather_fusion.1, pred[50]{0:T(512)(128)(4,1)S(1)} %copy-done.16, bf16[7,1,50,128,128]{4,3,2,1,0:T(8,128)(2,1)} %param.9), kind=kOutput, calls=%fused_computation.50 | convolution fusion | flops 421068800 | bytes 8192050 | tf_op jit(solution)/shard_map/qab,qbc->qac/dot_general | solution.py:36
  112.1 4.0 copy.47
  119.2 32.2 %all_to_all.71 = bf16[16,1,128,256]{3,2,1,0:T(8,128)(2,1)S(1)} all-to-all(bf16[16,1,128,256]{3,2,1,0:T(8,128)(2,1)S(1)} %copy.49), channel_id=1, replica_groups=mesh['row'=16,'col'=16] {'col'}, dimensions={0} | all-to-all | bytes 2097152 | tf_op jit(solution)/shard_map/all_to_all | solution.py:29
  154.3 3.8 all-to-all-start.4
  158.2 17.3 %all-to-all-done.4 = bf16[16,1,128,256]{3,2,1,0:T(8,128)(2,1)S(1)} async-done(((bf16[16,1,128,256]{3,2,1,0:T(8,128)(2,1)}), bf16[16,1,128,256]{3,2,1,0:T(8,128)(2,1)S(1)}, u32[]{:S(2)}, u32[]{:S(2)}) %all-to-all-start.4) | async-done | bytes 1048608 | tf_op jit(solution)/shard_map/all_to_all | solution.py:15
  178.0 5.3 %fusion.41 = bf16[50,128,256]{1,2,0:T(8,128)(2,1)} fusion(bf16[50,128,256]{2,1,0:T(8,128)(2,1)} %gather_fusion.2, pred[50]{0:T(512)(128)(4,1)S(1)} %copy-done.15, bf16[7,1,50,128,128]{4,3,2,1,0:T(8,128)(2,1)} %param.9), kind=kOutput, calls=%fused_computation.51 | convolution fusion | flops 421068800 | bytes 8192050 | tf_op jit(solution)/shard_map/qab,qbc->qac/dot_general | solution.py:36
  183.3 4.0 copy.52
  190.4 32.2 %all_to_all.72 = bf16[16,1,128,256]{3,2,1,0:T(8,128)(2,1)S(1)} all-to-all(bf16[16,1,128,256]{3,2,1,0:T(8,128)(2,1)S(1)} %copy.54), channel_id=1, replica_groups=mesh['row'=16,'col'=16] {'col'}, dimensions={0} | all-to-all | bytes 2097152 | tf_op jit(solution)/shard_map/all_to_all | solution.py:29
  229.2 17.3 %all-to-all-done.6 = bf16[16,1,128,256]{3,2,1,0:T(8,128)(2,1)S(1)} async-done(((bf16[16,1,128,256]{3,2,1,0:T(8,128)(2,1)}), bf16[16,1,128,256]{3,2,1,0:T(8,128)(2,1)S(1)}, u32[]{:S(2)}, u32[]{:S(2)}) %all-to-all-start.6) | async-done | bytes 1048608 | tf_op jit(solution)/shard_map/all_to_all | solution.py:15
  249.0 5.3 %fusion.44 = bf16[50,128,256]{1,2,0:T(8,128)(2,1)} fusion(bf16[50,128,256]{2,1,0:T(8,128)(2,1)} %gather_fusion.3, pred[50]{0:T(512)(128)(4,1)S(1)} %copy-done.14, bf16[7,1,50,128,128]{4,3,2,1,0:T(8,128)(2,1)} %param.9), kind=kOutput, calls=%fused_computation.52 | convolution fusion | flops 421068800 | bytes 8192050 | tf_op jit(solution)/shard_map/qab,qbc->qac/dot_general | solution.py:36
  254.3 4.0 copy.57
  261.2 32.2 %all_to_all.73 = bf16[16,1,128,256]{3,2,1,0:T(8,128)(2,1)S(1)} all-to-all(bf16[16,1,128,256]{3,2,1,0:T(8,128)(2,1)S(1)} %copy.59), channel_id=1, replica_groups=mesh['row'=16,'col'=16] {'col'}, dimensions={0} | all-to-all | bytes 2097152 | tf_op jit(solution)/shard_map/all_to_all | solution.py:29
  296.3 3.9 all-to-all-start.8
  300.2 17.3 %all-to-all-done.8 = bf16[16,1,128,256]{3,2,1,0:T(8,128)(2,1)S(1)} async-done(((bf16[16,1,128,256]{3,2,1,0:T(8,128)(2,1)}), bf16[16,1,128,256]{3,2,1,0:T(8,128)(2,1)S(1)}, u32[]{:S(2)}, u32[]{:S(2)}) %all-to-all-start.8) | async-done | bytes 1048608 | tf_op jit(solution)/shard_map/all_to_all | solution.py:15
  320.0 5.3 %fusion.47 = bf16[50,128,256]{1,2,0:T(8,128)(2,1)} fusion(bf16[50,128,256]{2,1,0:T(8,128)(2,1)} %gather_fusion.4, pred[50]{0:T(512)(128)(4,1)S(1)} %copy-done.13, bf16[7,1,50,128,128]{4,3,2,1,0:T(8,128)(2,1)} %param.9), kind=kOutput, calls=%fused_computation.53 | convolution fusion | flops 421068800 | bytes 8192050 | tf_op jit(solution)/shard_map/qab,qbc->qac/dot_general | solution.py:36
  325.3 4.0 copy.62
  332.1 32.2 %all_to_all.74 = bf16[16,1,128,256]{3,2,1,0:T(8,128)(2,1)S(1)} all-to-all(bf16[16,1,128,256]{3,2,1,0:T(8,128)(2,1)S(1)} %copy.64), channel_id=1, replica_groups=mesh['row'=16,'col'=16] {'col'}, dimensions={0} | all-to-all | bytes 2097152 | tf_op jit(solution)/shard_map/all_to_all | solution.py:29
  370.9 17.3 %all-to-all-done.10 = bf16[16,1,128,256]{3,2,1,0:T(8,128)(2,1)S(1)} async-done(((bf16[16,1,128,256]{3,2,1,0:T(8,128)(2,1)}), bf16[16,1,128,256]{3,2,1,0:T(8,128)(2,1)S(1)}, u32[]{:S(2)}, u32[]{:S(2)}) %all-to-all-start.10) | async-done | bytes 1048608 | tf_op jit(solution)/shard_map/all_to_all | solution.py:15
  390.7 5.3 %fusion.50 = bf16[50,128,256]{1,2,0:T(8,128)(2,1)} fusion(bf16[50,128,256]{2,1,0:T(8,128)(2,1)} %gather_fusion.5, pred[50]{0:T(512)(128)(4,1)S(1)} %copy-done.12, bf16[7,1,50,128,128]{4,3,2,1,0:T(8,128)(2,1)} %param.9), kind=kOutput, calls=%fused_computation.54 | convolution fusion | flops 421068800 | bytes 8192050 | tf_op jit(solution)/shard_map/qab,qbc->qac/dot_general | solution.py:36
  396.0 4.0 copy.67
  402.9 32.2 %all_to_all.75 = bf16[16,1,128,256]{3,2,1,0:T(8,128)(2,1)S(1)} all-to-all(bf16[16,1,128,256]{3,2,1,0:T(8,128)(2,1)S(1)} %copy.69), channel_id=1, replica_groups=mesh['row'=16,'col'=16] {'col'}, dimensions={0} | all-to-all | bytes 2097152 | tf_op jit(solution)/shard_map/all_to_all | solution.py:29
  438.0 3.9 all-to-all-start.12
  441.9 17.3 %all-to-all-done.12 = bf16[16,1,128,256]{3,2,1,0:T(8,128)(2,1)S(1)} async-done(((bf16[16,1,128,256]{3,2,1,0:T(8,128)(2,1)}), bf16[16,1,128,256]{3,2,1,0:T(8,128)(2,1)S(1)}, u32[]{:S(2)}, u32[]{:S(2)}) %all-to-all-start.12) | async-done | bytes 1048608 | tf_op jit(solution)/shard_map/all_to_all | solution.py:15
  461.7 5.3 %fusion.53 = bf16[50,128,256]{1,2,0:T(8,128)(2,1)} fusion(bf16[50,128,256]{2,1,0:T(8,128)(2,1)} %gather_fusion.6, pred[50]{0:T(512)(128)(4,1)S(1)} %copy-done.11, bf16[7,1,50,128,128]{4,3,2,1,0:T(8,128)(2,1)} %param.9), kind=kOutput, calls=%fused_computation.55 | convolution fusion | flops 421068800 | bytes 8192050 | tf_op jit(solution)/shard_map/qab,qbc->qac/dot_general | solution.py:36
  467.0 4.0 copy.72
  473.8 32.2 %all_to_all.76 = bf16[16,1,128,256]{3,2,1,0:T(8,128)(2,1)S(1)} all-to-all(bf16[16,1,128,256]{3,2,1,0:T(8,128)(2,1)S(1)} %copy.74), channel_id=1, replica_groups=mesh['row'=16,'col'=16] {'col'}, dimensions={0} | all-to-all | bytes 2097152 | tf_op jit(solution)/shard_map/all_to_all | solution.py:29
  (96 shorter events, 71.7 us)
Async XLA Ops:
  0.0 10.4 %copy-start.2 = (s32[7,1,50]{2,1,0:T(1,128)S(1)}, s32[7,1,50]{2,1,0:T(1,128)}, u32[]{:S(2)}) copy-start(s32[7,1,50]{2,1,0:T(1,128)} %param.10) | copy-start | bytes 4204
  0.0 11.0 %copy-start.1 = (s32[7,1,50]{2,1,0:T(1,128)S(1)}, s32[7,1,50]{2,1,0:T(1,128)}, u32[]{:S(2)}) copy-start(s32[7,1,50]{2,1,0:T(1,128)} %param.11) | copy-start | bytes 4204
  2.8 23.3 %all-to-all-start = ((bf16[16,1,128,256]{3,2,1,0:T(8,128)(2,1)}), bf16[16,1,128,256]{3,2,1,0:T(8,128)(2,1)S(1)}, u32[]{:S(2)}, u32[]{:S(2)}) async-start(bf16[16,1,128,256]{3,2,1,0:T(8,128)(2,1)} %broadcast_in_dim.25), calls=%async_computation | async-start | bytes 2097152 | tf_op jit(solution)/shard_map/all_to_all | solution.py:15
  40.3 40.3 %copy-start = (bf16[1,1,8,128,128]{4,3,2,1,0:T(8,128)(2,1)S(1)}, bf16[1,1,8,128,128]{4,3,2,1,0:T(8,128)(2,1)}, u32[]{:S(2)}) copy-start(bf16[1,1,8,128,128]{4,3,2,1,0:T(8,128)(2,1)} %param.8) | copy-start | bytes 786436
  40.7 46.3 %copy-start.10 = (s32[50]{0:T(128)S(1)}, s32[50]{0:T(128)}, u32[]{:S(2)}) copy-start(s32[50]{0:T(128)} %get-tuple-element.34) | copy-start | bytes 604
  83.3 21.0 %all-to-all-start.2 = ((bf16[16,1,128,256]{3,2,1,0:T(8,128)(2,1)}), bf16[16,1,128,256]{3,2,1,0:T(8,128)(2,1)S(1)}, u32[]{:S(2)}, u32[]{:S(2)}) async-start(bf16[16,1,128,256]{3,2,1,0:T(8,128)(2,1)} %broadcast_in_dim.26), calls=%async_computation.2 | async-start | bytes 2097152 | tf_op jit(solution)/shard_map/all_to_all | solution.py:15
  104.3 2.5 copy-start.16
  116.2 0.6 copy-start.4
  119.2 39.0 %copy-start.9 = (s32[50]{0:T(128)S(1)}, s32[50]{0:T(128)}, u32[]{:S(2)}) copy-start(s32[50]{0:T(128)} %get-tuple-element.32) | copy-start | bytes 604
  154.3 21.1 %all-to-all-start.4 = ((bf16[16,1,128,256]{3,2,1,0:T(8,128)(2,1)}), bf16[16,1,128,256]{3,2,1,0:T(8,128)(2,1)S(1)}, u32[]{:S(2)}, u32[]{:S(2)}) async-start(bf16[16,1,128,256]{3,2,1,0:T(8,128)(2,1)} %broadcast_in_dim.27), calls=%async_computation.4 | async-start | bytes 2097152 | tf_op jit(solution)/shard_map/all_to_all | solution.py:15
  175.5 2.5 copy-start.15
  187.3 0.7 copy-start.3
  190.4 38.8 %copy-start.8 = (s32[50]{0:T(128)S(1)}, s32[50]{0:T(128)}, u32[]{:S(2)}) copy-start(s32[50]{0:T(128)} %get-tuple-element.30) | copy-start | bytes 604
  225.5 21.0 %all-to-all-start.6 = ((bf16[16,1,128,256]{3,2,1,0:T(8,128)(2,1)}), bf16[16,1,128,256]{3,2,1,0:T(8,128)(2,1)S(1)}, u32[]{:S(2)}, u32[]{:S(2)}) async-start(bf16[16,1,128,256]{3,2,1,0:T(8,128)(2,1)} %broadcast_in_dim.50), calls=%async_computation.6 | async-start | bytes 2097152 | tf_op jit(solution)/shard_map/all_to_all | solution.py:15
  246.5 2.5 copy-start.14
  261.2 39.0 %copy-start.7 = (s32[50]{0:T(128)S(1)}, s32[50]{0:T(128)}, u32[]{:S(2)}) copy-start(s32[50]{0:T(128)} %get-tuple-element.28) | copy-start | bytes 604
  296.3 21.2 %all-to-all-start.8 = ((bf16[16,1,128,256]{3,2,1,0:T(8,128)(2,1)}), bf16[16,1,128,256]{3,2,1,0:T(8,128)(2,1)S(1)}, u32[]{:S(2)}, u32[]{:S(2)}) async-start(bf16[16,1,128,256]{3,2,1,0:T(8,128)(2,1)} %broadcast_in_dim.51), calls=%async_computation.8 | async-start | bytes 2097152 | tf_op jit(solution)/shard_map/all_to_all | solution.py:15
  317.4 2.5 copy-start.13
  332.1 38.8 %copy-start.6 = (s32[50]{0:T(128)S(1)}, s32[50]{0:T(128)}, u32[]{:S(2)}) copy-start(s32[50]{0:T(128)} %get-tuple-element.38) | copy-start | bytes 604
  367.2 21.0 %all-to-all-start.10 = ((bf16[16,1,128,256]{3,2,1,0:T(8,128)(2,1)}), bf16[16,1,128,256]{3,2,1,0:T(8,128)(2,1)S(1)}, u32[]{:S(2)}, u32[]{:S(2)}) async-start(bf16[16,1,128,256]{3,2,1,0:T(8,128)(2,1)} %broadcast_in_dim.52), calls=%async_computation.10 | async-start | bytes 2097152 | tf_op jit(solution)/shard_map/all_to_all | solution.py:15
  388.2 2.5 copy-start.12
  402.8 39.0 %copy-start.5 = (s32[50]{0:T(128)S(1)}, s32[50]{0:T(128)}, u32[]{:S(2)}) copy-start(s32[50]{0:T(128)} %get-tuple-element.7) | copy-start | bytes 604
  438.0 21.2 %all-to-all-start.12 = ((bf16[16,1,128,256]{3,2,1,0:T(8,128)(2,1)}), bf16[16,1,128,256]{3,2,1,0:T(8,128)(2,1)S(1)}, u32[]{:S(2)}, u32[]{:S(2)}) async-start(bf16[16,1,128,256]{3,2,1,0:T(8,128)(2,1)} %broadcast_in_dim.53), calls=%async_computation.12 | async-start | bytes 2097152 | tf_op jit(solution)/shard_map/all_to_all | solution.py:15
  459.2 2.5 copy-start.11
where the time goes:
time: 518 us; the launch traced here: 508 us
  blocking collectives  233 us (45%)
  waiting for transfers between devices  118 us (23%)
  matrix products  65 us (13%)
  local copies, waits for them, and re-layouts  59.4 us (11%)
  starting transfers between devices  30.1 us (6%)
    all_to_all x7, blocking collectives, sent_and_summed(): lax.all_to_all(parts, axis, split_axis=0, concat_axis=0, tiled=True)  233 us
    all_to_all x7, waiting for transfers between devices, sent_to_all(): return lax.all_to_all(copies, axis, split_axis=0, concat_axis=0, tiled=True)  118 us
    dot_general x7, matrix products, local_update(): jnp.einsum('qab,qbc->qac', panel, picked, preferred_element_type=jnp.floa...  37.2 us
    all_to_all x7, starting transfers between devices, sent_to_all(): return lax.all_to_all(copies, axis, split_axis=0, concat_axis=0, tiled=True)  30.1 us
    dot_general x7, local copies, waits for them, and re-layouts, local_update(): jnp.einsum('qab,qbc->qac', panel, picked, preferred_element_type=jnp.floa...  28.1 us
    gather x7, local copies, waits for them, and re-layouts, local_update(): picked = jnp.take(segment, source, axis=0)  17.6 us
    dot_general x7, matrix products, local_update(): sums = jnp.dot(onehot, prods.reshape(prods.shape[0], -1))  14.6 us
    dot_general x8, matrix products, local(): jnp.dot(diag_inverse[0, 0, section], current.astype(jnp.bfloat16), prefer...  13.2 us
  transfers between devices with their start and end apart: 7, of which 7 were waited for; matrix products, arithmetic and copies ran while one was open for 0% of the time, Pallas kernels for 0%

commit v1 on v0

v1 whole, which is shorter than its diff:
```python
import functools
import math

import jax
import jax.numpy as jnp
from jax import lax
from jax.experimental import pallas as pl
from jax.experimental.pallas import tpu as pltpu
from jax.sharding import PartitionSpec as P

MESH = pl.DeviceIdType.MESH
CORES = 2
CHUNKS = 4
VMEM_LIMIT = 60 * 1024 * 1024


def pair_slots(tiles, columns):
    return (tiles + columns) // 2


def tile_tables(source, target, rows, columns):
    levels, tiles = target.shape
    pairs = pair_slots(tiles, columns)
    tile_ids = jnp.arange(tiles, dtype=jnp.int32)
    target_ids = jnp.arange(columns, dtype=jnp.int32)
    hits = (target[:, :, None] == target_ids).astype(jnp.int32)
    count = hits.sum(axis=1)
    need = (count + 1) // 2
    base = jnp.where(target_ids[:, None] < target_ids[None, :], need[:, :, None], 0).sum(axis=1)
    earlier = (target[:, None, :] == target[:, :, None]) & (tile_ids[None, :] < tile_ids[:, None])
    place = 2 * (hits * base[:, None, :]).sum(axis=2) + earlier.astype(jnp.int32).sum(axis=2)
    filled = (place[:, None, :] == jnp.arange(2 * pairs, dtype=jnp.int32)[:, None]).astype(jnp.int32)
    slot_tile = (filled * tile_ids).sum(axis=2)
    slot_source = (filled * (source[:, None, :] - rows)).sum(axis=2) + rows
    opens = (base[:, None, :] == jnp.arange(pairs, dtype=jnp.int32)[:, None]) & (need[:, None, :] > 0)
    keep = 1 - opens.astype(jnp.int32).max(axis=2)
    last = jnp.where(need > 0, base + need - 1, pairs)
    return jnp.concatenate([slot_tile, slot_source, keep, last], axis=1)


def torus_order(rows):
    side = math.isqrt(rows)
    steps = [(dx, dy) for dx in range(side) for dy in range(side) if dx or dy]

    def far(step):
        return -sum(min(part, side - part) for part in step)

    return side, sorted(steps, key=far)


def ring_order(length):
    return sorted(range(1, length), key=lambda step: -min(step, length - step))


def kernel(
    rows, columns, levels, chunks, pairs,
    table, rhs_hbm, diag_hbm, panels_hbm, out,
    rhs, diag, panels, gathered, given, kept, traded, passed, arrived, work, runs, current,
    load_sem, panel_sem, gather_send, gather_recv, trade_send, trade_recv, pass_send, pass_recv,
):
    me_row, me_col = lax.axis_index("row"), lax.axis_index("col")
    floors = columns // CORES
    floor, core = me_col // CORES, lax.rem(me_col, CORES)
    side, row_steps = torus_order(rows)
    me_x, me_y = me_row // side, lax.rem(me_row, side)
    moves = (levels - 1) * chunks
    slots = 2 * pairs
    width = rhs.shape[1]

    def row_peer(step):
        return lax.rem(me_x + step[0], side) * side + lax.rem(me_y + step[1], side)

    def floor_peer(step):
        return lax.rem(floor + step, floors)

    partner = floor * CORES + 1 - core

    loads = [
        pltpu.make_async_copy(rhs_hbm, rhs, load_sem.at[0]),
        pltpu.make_async_copy(diag_hbm, diag, load_sem.at[1]),
    ]
    panel_loads = [
        pltpu.make_async_copy(panels_hbm.at[level], panels.at[level], panel_sem.at[level])
        for level in range(levels - 1)
    ]
    for load in loads + panel_loads:
        load.start()

    barrier = pltpu.get_barrier_semaphore()
    for step in row_steps:
        pl.semaphore_signal(barrier, inc=1, device_id=(row_peer(step), me_col), device_id_type=MESH)
    for step in ring_order(floors):
        pl.semaphore_signal(
            barrier, inc=1, device_id=(me_row, floor_peer(step) * CORES + core), device_id_type=MESH
        )
    pl.semaphore_signal(barrier, inc=1, device_id=(me_row, partner), device_id_type=MESH)

    work[rows] = jnp.zeros_like(work[rows])
    runs[pairs] = jnp.zeros_like(runs[pairs])
    for load in loads:
        load.wait()
    pl.semaphore_wait(barrier, rows - 1 + floors - 1 + 1)

    def landed(ref, sem):
        pltpu.make_async_copy(ref, ref, sem).wait()

    def solve(g):
        level = g // chunks
        current[...] = rhs[g].astype(jnp.float32)

        @pl.when(g >= chunks)
        def _():
            h = g - chunks
            landed(arrived.at[h, pl.ds(0, floors - 1)], pass_recv.at[h])
            incoming = arrived[h, 0].astype(jnp.float32)
            for z in range(1, floors):
                incoming = incoming + arrived[h, z].astype(jnp.float32)
            current[...] = current[...] - incoming

        block = lax.dot_general(
            current[...].astype(jnp.bfloat16), diag[level],
            (((1,), (1,)), ((), ())), preferred_element_type=jnp.float32,
        )

        @pl.when(g < moves)
        def _():
            gathered[g, me_row] = block.astype(jnp.bfloat16)
            for step in row_steps:
                pltpu.make_async_remote_copy(
                    src_ref=gathered.at[g, me_row],
                    dst_ref=gathered.at[g, me_row],
                    send_sem=gather_send.at[g],
                    recv_sem=gather_recv.at[g],
                    device_id=(row_peer(step), me_col),
                    device_id_type=MESH,
                ).start()

        out[g] = block

    def multiply(h):
        level = h // chunks

        @pl.when(h == 0)
        def _():
            for load in panel_loads:
                load.wait()

        landed(gathered.at[h, pl.ds(0, rows - 1)], gather_recv.at[h])
        for row in range(rows):
            work[row] = gathered[h, row]
        total = jnp.zeros((width, rhs.shape[2]), jnp.float32)
        for pair in range(pairs):
            first, second = 2 * pair, 2 * pair + 1
            picked = jnp.concatenate(
                [work[table[level, slots + first]], work[table[level, slots + second]]], axis=1
            )
            tile = jnp.concatenate(
                [panels[level, table[level, first]], panels[level, table[level, second]]], axis=1
            )
            product = lax.dot_general(
                picked, tile, (((1,), (1,)), ((), ())), preferred_element_type=jnp.float32
            )
            total = product + jnp.where(table[level, 2 * slots + pair] != 0, total, 0.0)
            runs[pair] = total.astype(jnp.bfloat16)
        lasts = 2 * slots + pairs
        for z in range(floors):
            given[h, z] = runs[table[level, lasts + CORES * z + 1 - core]]
        pltpu.make_async_remote_copy(
            src_ref=given.at[h],
            dst_ref=traded.at[h],
            send_sem=trade_send.at[h],
            recv_sem=trade_recv.at[h],
            device_id=(me_row, partner),
            device_id_type=MESH,
        ).start()
        for z in range(floors):
            kept[h, z] = runs[table[level, lasts + CORES * z + core]]

    def exchange(h):
        landed(traded.at[h], trade_recv.at[h])

        def both(z):
            return (kept[h, z].astype(jnp.float32) + traded[h, z].astype(jnp.float32)).astype(jnp.bfloat16)

        for step in ring_order(floors):
            z = floor_peer(step)
            passed[h, z] = both(z)
            pltpu.make_async_remote_copy(
                src_ref=passed.at[h, z],
                dst_ref=arrived.at[h, floor],
                send_sem=pass_send.at[h],
                recv_sem=pass_recv.at[h],
                device_id=(me_row, z * CORES + core),
                device_id_type=MESH,
            ).start()
        arrived[h, floor] = both(floor)

    late_product = 1 if chunks >= 4 else 0
    late_exchange = 2 if chunks >= 4 else min(1, chunks - 1)

    def stage(run, h):
        @pl.when((h >= 0) & (h < moves))
        def _():
            run(h)

    def turn(g, carry):
        solve(g)
        if late_product == late_exchange:
            stage(multiply, g - late_product)
            stage(exchange, g - late_exchange)
        else:
            stage(exchange, g - late_exchange)
            stage(multiply, g - late_product)
        return carry

    lax.fori_loop(0, levels * chunks, turn, 0)

    def drain(h, carry):
        landed(gathered.at[h, pl.ds(0, rows - 1)], gather_send.at[h])
        landed(given.at[h], trade_send.at[h])
        landed(passed.at[h, pl.ds(0, floors - 1)], pass_send.at[h])
        return carry

    lax.fori_loop(0, moves, drain, 0)


def local(rows, columns, right_side, diag_inverse, panels, tile_source, tile_target):
    levels, depth, cols = right_side.shape[2:]
    tiles = panels.shape[2]
    chunks = CHUNKS
    width = cols // chunks
    pairs = pair_slots(tiles, columns)
    moves = (levels - 1) * chunks
    floors = columns // CORES
    table = tile_tables(tile_source[:, 0], tile_target[:, 0], rows, columns)
    rhs = jnp.swapaxes(right_side[0, 0], 1, 2).reshape(levels * chunks, width, depth)
    dma = pltpu.SemaphoreType.DMA
    anywhere = pl.BlockSpec(memory_space=pl.ANY)
    solved = pl.pallas_call(
        functools.partial(kernel, rows, columns, levels, chunks, pairs),
        out_shape=jax.ShapeDtypeStruct((levels * chunks, width, depth), jnp.float32),
        in_specs=[pl.BlockSpec(memory_space=pltpu.SMEM), anywhere, anywhere, anywhere],
        out_specs=pl.BlockSpec(memory_space=pltpu.VMEM),
        scratch_shapes=[
            pltpu.VMEM((levels * chunks, width, depth), jnp.bfloat16),
            pltpu.VMEM((levels, depth, depth), jnp.bfloat16),
            pltpu.VMEM((levels - 1, tiles, depth, depth), jnp.bfloat16),
            pltpu.VMEM((moves, rows, width, depth), jnp.bfloat16),
            pltpu.VMEM((moves, floors, width, depth), jnp.bfloat16),
            pltpu.VMEM((moves, floors, width, depth), jnp.bfloat16),
            pltpu.VMEM((moves, floors, width, depth), jnp.bfloat16),
            pltpu.VMEM((moves, floors, width, depth), jnp.bfloat16),
            pltpu.VMEM((moves, floors, width, depth), jnp.bfloat16),
            pltpu.VMEM((rows + 1, width, depth), jnp.bfloat16),
            pltpu.VMEM((pairs + 1, width, depth), jnp.bfloat16),
            pltpu.VMEM((width, depth), jnp.float32),
            dma((2,)),
            dma((levels - 1,)),
            dma((moves,)),
            dma((moves,)),
            dma((moves,)),
            dma((moves,)),
            dma((moves,)),
            dma((moves,)),
        ],
        compiler_params=pltpu.CompilerParams(
            collective_id=0, has_side_effects=True, vmem_limit_bytes=VMEM_LIMIT
        ),
        name="level_solve",
    )(table, rhs, diag_inverse[0, 0], panels[:, 0])
    solved = jnp.swapaxes(solved.reshape(levels, cols, depth), 1, 2)
    return solved[None, None]


def solution(mesh):
    return jax.shard_map(
        functools.partial(local, mesh.shape["row"], mesh.shape["col"]),
        mesh=mesh,
        in_specs=(
            P("row", "col", None, None, None),
            P("row", "col", None, None, None),
            P(None, "row", "col", None, None),
            P(None, "row", "col"),
            P(None, "row", "col"),
        ),
        out_specs=P("row", "col", None, None, None),
        check_vma=False,
    )
```

time: 518 us -> 129 us (0.25); the launches traced: 508 us -> 129 us
  blocking collectives: 233 us -> 0 us
  Pallas kernels: 0 us -> 122 us
  waiting for transfers between devices: 118 us -> 0 us
  matrix products: 65 us -> 0 us
  local copies, waits for them, and re-layouts: 59.4 us -> 5.26 us
  starting transfers between devices: 30.1 us -> 0 us
    all_to_all x7 -> x0, blocking collectives: 233 us -> none  [sent_and_summed(): lax.all_to_all(parts, axis, split_axis=0, concat_axis=0, tiled=True)]
    pallas_call x0 -> x1, Pallas kernels: none -> 122 us  [local(): pl.pallas_call(functools.partial(kernel, rows, columns, levels, chunks, p...]
    all_to_all x7 -> x0, waiting for transfers between devices: 118 us -> none  [sent_to_all(): return lax.all_to_all(copies, axis, split_axis=0, concat_axis=0, tiled=True)]
    dot_general x22 -> x0, matrix products: 65 us -> none  [the longest x7 37.2 us: local_update(): jnp.einsum('qab,qbc->qac', panel, picked, preferred_element_type=jnp.floa...]
    dot_general x14 -> x0, local copies, waits for them, and re-layouts: 30.7 us -> none  [the longest x7 28.1 us: local_update(): jnp.einsum('qab,qbc->qac', panel, picked, preferred_element_type=jnp.floa...]
    all_to_all x7 -> x0, starting transfers between devices: 30.1 us -> none  [sent_to_all(): return lax.all_to_all(copies, axis, split_axis=0, concat_axis=0, tiled=True)]
    gather x7 -> x0, local copies, waits for them, and re-layouts: 17.6 us -> none  [local_update(): picked = jnp.take(segment, source, axis=0)]
    broadcast_in_dim x7 -> x0, local copies, waits for them, and re-layouts: 7.56 us -> none  [sent_to_all(): copies = jnp.broadcast_to(x, (lax.axis_size(axis), *x.shape))]
  transfers between devices with their start and end apart: 7 -> 0, of which waited for: 7 -> 0; matrix products, arithmetic and copies ran while one was open for 0% -> 0% of each run, Pallas kernels for 0% -> 0%
where the time goes in v1:
time: 129 us
  Pallas kernels  122 us (95%)
  local copies, waits for them, and re-layouts  5.26 us (4%)
  other arithmetic  2.41 us (2%)
    pallas_call x1, Pallas kernels, local(): pl.pallas_call(functools.partial(kernel, rows, columns, levels, chunks, p...  122 us

profile of v1, /device:TPU:1, one launch (start us, length us, event | category | flops | bytes accessed | tf_op | source)
XLA Modules:
  0.0 129.4 jit_solution(10336890483142342416)
XLA Ops:
  0.0 0.7 broadcast_add_fusion.1
  0.7 0.7 copy.15
  1.4 0.2 convert_reduce_fusion.2
  1.6 0.1 select_reduce_fusion.3
  1.7 0.1 convert_reduce_fusion.1
  1.9 0.1 select_reduce_fusion.2
  2.0 0.3 convert_reduce_fusion
  2.3 0.2 select_reduce_fusion.1
  2.5 0.7 pad_add_fusion.table
  3.2 2.0 %copy.8 = bf16[8,256,128]{2,1,0:T(8,128)(2,1)} copy(bf16[8,256,128]{1,2,0:T(8,128)(2,1)} %bitcast.19) | data formatting | bytes 1048576 | tf_op jit(solution)/shard_map/transpose | solution.py:236
  5.2 121.7 %level_solve.1 = f32[32,64,128]{2,1,0:T(8,128)} custom-call(s32[7,181]{1,0:T(8,128)} %pad_add_fusion.table, bf16[32,64,128]{2,1,0:T(8,128)(2,1)} %bitcast.18, bf16[8,128,128]{2,1,0:T(8,128)(2,1)} %bitcast.20, bf16[7,50,128,128]{3,2,1,0:T(8,128)(2,1)} %bitcast.16), custom_call_target="tpu_custom_call" | custom-call | tf_op jit(solution)/shard_map/level_solve/pallas_call | solution.py:239
  126.9 2.5 %copy.9 = f32[8,256,128]{1,2,0:T(8,128)} copy(f32[8,256,128]{2,1,0:T(8,128)} %bitcast.17) | data formatting | bytes 2097152 | tf_op jit(solution)/shard_map/reshape | solution.py:271
  (8 shorter events, 0.1 us)

commit v2 on v1

v2 whole, which is shorter than its diff:
```python
import functools
import math

import jax
import jax.numpy as jnp
from jax import lax
from jax.experimental import pallas as pl
from jax.experimental.pallas import tpu as pltpu
from jax.sharding import PartitionSpec as P

MESH = pl.DeviceIdType.MESH
CORES = 2
CHUNKS = 8
LISTS = 4
LATE_PRODUCT = 3
LATE_EXCHANGE = 4
NT = (((1,), (1,)), ((), ()))
VMEM_LIMIT = 60 * 1024 * 1024


def ordered_tiles(source, target, rows, columns, tiles):
    lanes = source.shape[1]
    key = (target * lanes + lax.broadcasted_iota(jnp.int32, source.shape, 1)) * rows + source
    across = jnp.broadcast_to(key, (lanes, lanes))
    down = across.T
    place = jnp.sum((down < across).astype(jnp.int32), axis=0, keepdims=True)
    slot = lax.broadcasted_iota(jnp.int32, (lanes, lanes), 1)
    placed = jnp.broadcast_to(place, (lanes, lanes)).T == slot
    ordered = jnp.sum(jnp.where(placed, down, 0), axis=0, keepdims=True)
    ends = jnp.sum((down < (slot + 1) * (lanes * rows)).astype(jnp.int32), axis=0, keepdims=True)
    number = ordered // rows
    return [
        jnp.clip(lax.rem(number, lanes), 0, tiles - 1),
        jnp.clip(lax.rem(ordered, rows), 0, rows - 1),
        number // lanes,
        jnp.clip(ends, 0, tiles),
    ]


def torus_order(rows):
    side = math.isqrt(rows)
    steps = [(dx, dy) for dx in range(side) for dy in range(side) if dx or dy]

    def far(step):
        return -sum(min(part, side - part) for part in step)

    return side, sorted(steps, key=far)


def ring_order(length):
    return sorted(range(1, length), key=lambda step: -min(step, length - step))


def kernel(
    rows, columns, levels, chunks, tiles,
    source_ids, target_ids, rhs_hbm, diag_hbm, panels_hbm, out,
    table, lists, source_pad, target_pad, right, rhs, diag, panels, gathered, given, kept, traded, passed, arrived, work, runs, current,
    load_sem, table_sem, panel_sem, gather_send, gather_recv, trade_send, trade_recv, pass_send, pass_recv,
):
    me_row, me_col = lax.axis_index("row"), lax.axis_index("col")
    floors = columns // CORES
    floor, core = me_col // CORES, lax.rem(me_col, CORES)
    side, row_steps = torus_order(rows)
    me_x, me_y = me_row // side, lax.rem(me_row, side)
    moves = (levels - 1) * chunks
    width, depth = rhs.shape[1:]

    def row_peer(step):
        return lax.rem(me_x + step[0], side) * side + lax.rem(me_y + step[1], side)

    def floor_peer(step):
        return lax.rem(floor + step, floors)

    partner = floor * CORES + 1 - core

    loads = [
        pltpu.make_async_copy(rhs_hbm, right, load_sem.at[0]),
        pltpu.make_async_copy(diag_hbm, diag, load_sem.at[1]),
    ]
    panel_loads = [
        pltpu.make_async_copy(panels_hbm.at[level], panels.at[level], panel_sem.at[level])
        for level in range(levels - 1)
    ]
    for load in loads + panel_loads:
        load.start()

    barrier = pltpu.get_barrier_semaphore()
    for step in row_steps:
        pl.semaphore_signal(barrier, inc=1, device_id=(row_peer(step), me_col), device_id_type=MESH)
    for step in ring_order(floors):
        pl.semaphore_signal(
            barrier, inc=1, device_id=(me_row, floor_peer(step) * CORES + core), device_id_type=MESH
        )
    pl.semaphore_signal(barrier, inc=1, device_id=(me_row, partner), device_id_type=MESH)

    work[rows] = jnp.zeros_like(work[rows])
    runs[tiles] = jnp.zeros_like(runs[tiles])
    for load in loads:
        load.wait()
    with jax.named_scope("wait_barrier"):
        pl.semaphore_wait(barrier, rows - 1 + floors - 1 + 1)

    def turned(level):
        block = right[level].astype(jnp.float32).T
        rhs[pl.ds(level * chunks, chunks)] = block.reshape(chunks, width, depth)

    def plan():
        target_pad[...] = jnp.full_like(target_pad, columns)
        source_pad[...] = jnp.zeros_like(source_pad)
        target_pad[pl.ds(0, levels - 1), pl.ds(0, tiles)] = target_ids[...]
        source_pad[pl.ds(0, levels - 1), pl.ds(0, tiles)] = source_ids[...]
        for level in range(levels - 1):
            found = ordered_tiles(
                source_pad[pl.ds(level, 1)], target_pad[pl.ds(level, 1)], rows, columns, tiles
            )
            for place, values in enumerate(found):
                lists[pl.ds(LISTS * level + place, 1)] = values
        copy = pltpu.make_async_copy(lists, table, table_sem.at[0])
        copy.start()
        for level in range(1, levels):
            turned(level)
        copy.wait()

    def landed(ref, sem):
        pltpu.make_async_copy(ref, ref, sem).wait()

    def solve(g):
        level = g // chunks
        current[...] = rhs[g]

        @pl.when(g >= chunks)
        def _():
            h = g - chunks
            with jax.named_scope("wait_pass"):
                landed(arrived.at[h, pl.ds(0, floors - 1)], pass_recv.at[h])
            incoming = arrived[h, 0].astype(jnp.float32)
            for z in range(1, floors):
                incoming = incoming + arrived[h, z].astype(jnp.float32)
            current[...] = current[...] - incoming

        block = lax.dot_general(
            current[...].astype(jnp.bfloat16), diag[level],
            NT, preferred_element_type=jnp.float32,
        )

        @pl.when(g < moves)
        def _():
            gathered[g, me_row] = block.astype(jnp.bfloat16)
            for step in row_steps:
                pltpu.make_async_remote_copy(
                    src_ref=gathered.at[g, me_row],
                    dst_ref=gathered.at[g, me_row],
                    send_sem=gather_send.at[g],
                    recv_sem=gather_recv.at[g],
                    device_id=(row_peer(step), me_col),
                    device_id_type=MESH,
                ).start()

        out[g] = block

    def multiply(h):
        level = h // chunks

        @pl.when(h == 0)
        def _():
            for load in panel_loads:
                load.wait()

        with jax.named_scope("wait_gather"):
            landed(gathered.at[h, pl.ds(0, rows - 1)], gather_recv.at[h])
        for row in range(rows):
            work[row] = gathered[h, row]
        nothing = jnp.zeros((width, depth), jnp.bfloat16)
        total = jnp.zeros((width, depth), jnp.float32)
        before = -1
        for first in range(0, tiles, 2):
            second = first + 1
            tile = panels[level, table[LISTS * level, first]]
            block = work[table[LISTS * level + 1, first]]
            target = table[LISTS * level + 2, first]
            if second == tiles:
                product = lax.dot_general(block, tile, NT, preferred_element_type=jnp.float32)
                runs[first] = (product + jnp.where(target == before, total, 0.0)).astype(jnp.bfloat16)
                break
            tile = jnp.concatenate([tile, panels[level, table[LISTS * level, second]]], axis=1)
            source = table[LISTS * level + 1, second]
            same = table[LISTS * level + 2, second] == target
            picked = jnp.concatenate(
                [
                    jnp.concatenate([block, work[jnp.where(same, source, rows)]], axis=1),
                    jnp.concatenate([nothing, work[jnp.where(same, rows, source)]], axis=1),
                ],
                axis=0,
            )
            product = lax.dot_general(picked, tile, NT, preferred_element_type=jnp.float32)
            total = product[:width] + jnp.where(target == before, total, 0.0)
            runs[first] = total.astype(jnp.bfloat16)
            total = jnp.where(same, total, product[width:])
            runs[second] = total.astype(jnp.bfloat16)
            before = table[LISTS * level + 2, second]

        def summed(column):
            end = table[LISTS * level + 3, column]
            start = jnp.where(column == 0, 0, table[LISTS * level + 3, jnp.maximum(column - 1, 0)])
            return runs[jnp.where(end > start, end - 1, tiles)]

        for z in range(floors):
            given[h, z] = summed(CORES * z + 1 - core)
        pltpu.make_async_remote_copy(
            src_ref=given.at[h],
            dst_ref=traded.at[h],
            send_sem=trade_send.at[h],
            recv_sem=trade_recv.at[h],
            device_id=(me_row, partner),
            device_id_type=MESH,
        ).start()
        for z in range(floors):
            kept[h, z] = summed(CORES * z + core)

    def exchange(h):
        with jax.named_scope("wait_trade"):
            landed(traded.at[h], trade_recv.at[h])

        def both(z):
            return (kept[h, z].astype(jnp.float32) + traded[h, z].astype(jnp.float32)).astype(jnp.bfloat16)

        for step in ring_order(floors):
            z = floor_peer(step)
            passed[h, z] = both(z)
            pltpu.make_async_remote_copy(
                src_ref=passed.at[h, z],
                dst_ref=arrived.at[h, floor],
                send_sem=pass_send.at[h],
                recv_sem=pass_recv.at[h],
                device_id=(me_row, z * CORES + core),
                device_id_type=MESH,
            ).start()
        arrived[h, floor] = both(floor)

    def stage(run, h):
        @pl.when((h >= 0) & (h < moves))
        def _():
            with jax.named_scope(run.__name__):
                run(h)

    def turn(g, carry):
        @pl.when(g >= chunks)
        def _():
            with jax.named_scope("solve"):
                solve(g)

        stage(multiply, g - LATE_PRODUCT)
        stage(exchange, g - LATE_EXCHANGE)
        return carry

    def begin(g, carry):
        solve(g)
        return carry

    turned(0)
    lax.fori_loop(0, chunks, begin, 0)
    with jax.named_scope("plan"):
        plan()
    lax.fori_loop(0, levels * chunks, turn, 0)

    def drain(h, carry):
        landed(gathered.at[h, pl.ds(0, rows - 1)], gather_send.at[h])
        landed(given.at[h], trade_send.at[h])
        landed(passed.at[h, pl.ds(0, floors - 1)], pass_send.at[h])
        return carry

    lax.fori_loop(0, moves, drain, 0)


def local(rows, columns, right_side, diag_inverse, panels, tile_source, tile_target):
    levels, depth, cols = right_side.shape[2:]
    tiles = panels.shape[2]
    chunks = CHUNKS
    width = cols // chunks
    moves = (levels - 1) * chunks
    floors = columns // CORES
    lanes = -(-tiles // depth) * depth
    dma = pltpu.SemaphoreType.DMA
    anywhere = pl.BlockSpec(memory_space=pl.ANY)
    solved = pl.pallas_call(
        functools.partial(kernel, rows, columns, levels, chunks, tiles),
        out_shape=jax.ShapeDtypeStruct((levels * chunks, width, depth), jnp.float32),
        in_specs=[pl.BlockSpec(memory_space=pltpu.VMEM)] * 2 + [anywhere] * 3,
        out_specs=pl.BlockSpec(memory_space=pltpu.VMEM),
        scratch_shapes=[
            pltpu.SMEM((LISTS * levels, lanes), jnp.int32),
            pltpu.VMEM((LISTS * levels, lanes), jnp.int32),
            pltpu.VMEM((levels, lanes), jnp.int32),
            pltpu.VMEM((levels, lanes), jnp.int32),
            pltpu.VMEM((levels, depth, cols), jnp.bfloat16),
            pltpu.VMEM((levels * chunks, width, depth), jnp.float32),
            pltpu.VMEM((levels, depth, depth), jnp.bfloat16),
            pltpu.VMEM((levels - 1, tiles, depth, depth), jnp.bfloat16),
            pltpu.VMEM((moves, rows, width, depth), jnp.bfloat16),
            pltpu.VMEM((moves, floors, width, depth), jnp.bfloat16),
            pltpu.VMEM((moves, floors, width, depth), jnp.bfloat16),
            pltpu.VMEM((moves, floors, width, depth), jnp.bfloat16),
            pltpu.VMEM((moves, floors, width, depth), jnp.bfloat16),
            pltpu.VMEM((moves, floors, width, depth), jnp.bfloat16),
            pltpu.VMEM((rows + 1, width, depth), jnp.bfloat16),
            pltpu.VMEM((tiles + 1, width, depth), jnp.bfloat16),
            pltpu.VMEM((width, depth), jnp.float32),
            dma((2,)),
            dma((1,)),
            dma((levels - 1,)),
            dma((moves,)),
            dma((moves,)),
            dma((moves,)),
            dma((moves,)),
            dma((moves,)),
            dma((moves,)),
        ],
        compiler_params=pltpu.CompilerParams(
            collective_id=0, has_side_effects=True, vmem_limit_bytes=VMEM_LIMIT
        ),
        name="level_solve",
    )(tile_source[:, 0], tile_target[:, 0], right_side[0, 0], diag_inverse[0, 0], panels[:, 0])
    solved = jnp.swapaxes(solved.reshape(levels, cols, depth), 1, 2)
    return solved[None, None]


def solution(mesh):
    return jax.shard_map(
        functools.partial(local, mesh.shape["row"], mesh.shape["col"]),
        mesh=mesh,
        in_specs=(
            P("row", "col", None, None, None),
            P("row", "col", None, None, None),
            P(None, "row", "col", None, None),
            P(None, "row", "col"),
            P(None, "row", "col"),
        ),
        out_specs=P("row", "col", None, None, None),
        check_vma=False,
    )
```

time: 129 us -> 117 us (0.907)
  Pallas kernels: 122 us -> 113 us
  other arithmetic: 2.41 us -> 0 us
  local copies, waits for them, and re-layouts: 5.26 us -> 3.83 us
    pallas_call x1, Pallas kernels: 122 us -> 113 us  [local(): pl.pallas_call(functools.partial(kernel, rows, columns, levels, chunks, t...]
    transpose x1 -> x0, local copies, waits for them, and re-layouts: 2.04 us -> none  [local(): jnp.swapaxes(right_side[0, 0], 1, 2).reshape(levels * chunks, width, depth)]
where the time goes in v2:
time: 117 us; the launch traced here: 116 us
  Pallas kernels  113 us (97%)
  local copies, waits for them, and re-layouts  3.83 us (3%)
    pallas_call x1, Pallas kernels, local(): pl.pallas_call(functools.partial(kernel, rows, columns, levels, chunks, t...  113 us
    reshape x1, local copies, waits for them, and re-layouts, local(): solved = jnp.swapaxes(solved.reshape(levels, cols, depth), 1, 2)  2.53 us

profile of v2, /device:TPU:1, one launch (start us, length us, event | category | flops | bytes accessed | tf_op | source)
XLA Modules:
  0.0 116.5 jit_solution(13860717519768943206)
XLA Ops:
  0.0 1.3 %copy_bitcast_fusion = (s32[7,50]{1,0:T(8,128)}, s32[7,50]{1,0:T(8,128)}) fusion(s32[7,1,50]{2,1,0:T(1,128)} %param.9, s32[7,1,50]{2,1,0:T(1,128)} %param.8), kind=kLoop, calls=%fused_computation | loop fusion | bytes 5600
  1.3 112.6 %level_solve.1 = f32[64,32,128]{2,1,0:T(8,128)} custom-call(s32[7,50]{1,0:T(8,128)} %get-tuple-element.6.source_ids, s32[7,50]{1,0:T(8,128)} %get-tuple-element.5.target_ids, bf16[8,128,256]{2,1,0:T(8,128)(2,1)} %bitcast.13, bf16[8,128,128]{2,1,0:T(8,128)(2,1)} %bitcast.14, bf16[7,50,128,128]{3,2,1,0:T(8,128)(2,1)} %bitcast.11), custom_call_target="tpu_custom_call" | custom-call | tf_op jit(solution)/shard_map/level_solve/pallas_call | solution.py:285
  113.9 2.5 %copy.6 = f32[8,256,128]{1,2,0:T(8,128)} copy(f32[8,256,128]{2,1,0:T(8,128)} %bitcast.12) | data formatting | bytes 2097152 | tf_op jit(solution)/shard_map/reshape | solution.py:323

commit v3 on v2

--- a/solution.py
+++ b/solution.py
@@ -53,9 +53,9 @@
 
 def kernel(
     rows, columns, levels, chunks, tiles,
-    source_ids, target_ids, rhs_hbm, diag_hbm, panels_hbm, out,
-    table, lists, source_pad, target_pad, right, rhs, diag, panels, gathered, given, kept, traded, passed, arrived, work, runs, current,
-    load_sem, table_sem, panel_sem, gather_send, gather_recv, trade_send, trade_recv, pass_send, pass_recv,
+    source_hbm, target_hbm, rhs_hbm, diag_hbm, panels_hbm, out_hbm,
+    source_ids, target_ids, out, straight, table, lists, source_pad, target_pad, right, rhs, diag, panels, gathered, given, kept, traded, passed, arrived, work, runs, current,
+    out_sem, load_sem, table_sem, panel_sem, gather_send, gather_recv, trade_send, trade_recv, pass_send, pass_recv,
 ):
     me_row, me_col = lax.axis_index("row"), lax.axis_index("col")
     floors = columns // CORES
@@ -77,11 +77,15 @@
         pltpu.make_async_copy(rhs_hbm, right, load_sem.at[0]),
         pltpu.make_async_copy(diag_hbm, diag, load_sem.at[1]),
     ]
+    id_loads = [
+        pltpu.make_async_copy(source_hbm, source_ids, load_sem.at[2]),
+        pltpu.make_async_copy(target_hbm, target_ids, load_sem.at[3]),
+    ]
     panel_loads = [
         pltpu.make_async_copy(panels_hbm.at[level], panels.at[level], panel_sem.at[level])
         for level in range(levels - 1)
     ]
-    for load in loads + panel_loads:
+    for load in loads + id_loads + panel_loads:
         load.start()
 
     barrier = pltpu.get_barrier_semaphore()
@@ -100,6 +104,14 @@
     with jax.named_scope("wait_barrier"):
         pl.semaphore_wait(barrier, rows - 1 + floors - 1 + 1)
 
+    def leave(level):
+        return pltpu.make_async_copy(straight.at[level], out_hbm.at[level], out_sem.at[level])
+
+    def finish(level):
+        block = out[pl.ds(level * chunks, chunks)].reshape(chunks * width, depth)
+        straight[level] = block.T
+        leave(level).start()
+
     def turned(level):
         block = right[level].astype(jnp.float32).T
         rhs[pl.ds(level * chunks, chunks)] = block.reshape(chunks, width, depth)
@@ -107,8 +119,11 @@
     def plan():
         target_pad[...] = jnp.full_like(target_pad, columns)
         source_pad[...] = jnp.zeros_like(source_pad)
-        target_pad[pl.ds(0, levels - 1), pl.ds(0, tiles)] = target_ids[...]
-        source_pad[pl.ds(0, levels - 1), pl.ds(0, tiles)] = source_ids[...]
+        for load in id_loads:
+            load.wait()
+        for level in range(levels - 1):
+            target_pad[pl.ds(level, 1), pl.ds(0, tiles)] = target_ids[level]
+            source_pad[pl.ds(level, 1), pl.ds(0, tiles)] = source_ids[level]
         for level in range(levels - 1):
             found = ordered_tiles(
                 source_pad[pl.ds(level, 1)], target_pad[pl.ds(level, 1)], rows, columns, tiles
@@ -244,13 +259,19 @@
                 run(h)
 
     def turn(g, carry):
-        @pl.when(g >= chunks)
+        @pl.when(g > LATE_PRODUCT)
         def _():
             with jax.named_scope("solve"):
                 solve(g)
 
         stage(multiply, g - LATE_PRODUCT)
         stage(exchange, g - LATE_EXCHANGE)
+
+        @pl.when(lax.rem(g, chunks) == chunks - 1)
+        def _():
+            with jax.named_scope("finish"):
+                finish(g // chunks)
+
         return carry
 
     def begin(g, carry):
@@ -258,7 +279,7 @@
         return carry
 
     turned(0)
-    lax.fori_loop(0, chunks, begin, 0)
+    lax.fori_loop(0, LATE_PRODUCT + 1, begin, 0)
     with jax.named_scope("plan"):
         plan()
     lax.fori_loop(0, levels * chunks, turn, 0)
@@ -270,6 +291,8 @@
         return carry
 
     lax.fori_loop(0, moves, drain, 0)
+    for level in range(levels):
+        leave(level).wait()
 
 
 def local(rows, columns, right_side, diag_inverse, panels, tile_source, tile_target):
@@ -284,10 +307,14 @@
     anywhere = pl.BlockSpec(memory_space=pl.ANY)
     solved = pl.pallas_call(
         functools.partial(kernel, rows, columns, levels, chunks, tiles),
-        out_shape=jax.ShapeDtypeStruct((levels * chunks, width, depth), jnp.float32),
-        in_specs=[pl.BlockSpec(memory_space=pltpu.VMEM)] * 2 + [anywhere] * 3,
-        out_specs=pl.BlockSpec(memory_space=pltpu.VMEM),
+        out_shape=jax.ShapeDtypeStruct((levels, depth, cols), jnp.float32),
+        in_specs=[anywhere] * 5,
+        out_specs=anywhere,
         scratch_shapes=[
+            pltpu.VMEM((levels - 1, 1, tiles), jnp.int32),
+            pltpu.VMEM((levels - 1, 1, tiles), jnp.int32),
+            pltpu.VMEM((levels * chunks, width, depth), jnp.float32),
+            pltpu.VMEM((levels, depth, cols), jnp.float32),
             pltpu.SMEM((LISTS * levels, lanes), jnp.int32),
             pltpu.VMEM((LISTS * levels, lanes), jnp.int32),
             pltpu.VMEM((levels, lanes), jnp.int32),
@@ -305,7 +332,8 @@
             pltpu.VMEM((rows + 1, width, depth), jnp.bfloat16),
             pltpu.VMEM((tiles + 1, width, depth), jnp.bfloat16),
             pltpu.VMEM((width, depth), jnp.float32),
-            dma((2,)),
+            dma((levels,)),
+            dma((4,)),
             dma((1,)),
             dma((levels - 1,)),
             dma((moves,)),
@@ -319,8 +347,7 @@
             collective_id=0, has_side_effects=True, vmem_limit_bytes=VMEM_LIMIT
         ),
         name="level_solve",
-    )(tile_source[:, 0], tile_target[:, 0], right_side[0, 0], diag_inverse[0, 0], panels[:, 0])
-    solved = jnp.swapaxes(solved.reshape(levels, cols, depth), 1, 2)
+    )(tile_source, tile_target, right_side[0, 0], diag_inverse[0, 0], panels[:, 0])
     return solved[None, None]
 
 

time: 117 us -> 113 us (0.966)
  Pallas kernels: 113 us -> 111 us
  local copies, waits for them, and re-layouts: 3.83 us -> 2.27 us
    reshape x1 -> x0, local copies, waits for them, and re-layouts: 2.53 us -> none  [local(): solved = jnp.swapaxes(solved.reshape(levels, cols, depth), 1, 2)]
    pallas_call x1, Pallas kernels: 113 us -> 111 us  [local(): pl.pallas_call(functools.partial(kernel, rows, columns, levels, chunks, t...]
where the time goes in v3:
time: 113 us
  Pallas kernels  111 us (98%)
  local copies, waits for them, and re-layouts  2.27 us (2%)
    pallas_call x1, Pallas kernels, local(): pl.pallas_call(functools.partial(kernel, rows, columns, levels, chunks, t...  111 us
    unnamed x1, local copies, waits for them, and re-layouts  2.27 us

profile of v3, /device:TPU:1, one launch (start us, length us, event | category | flops | bytes accessed | tf_op | source)
XLA Modules:
  0.0 113.3 jit_solution(2782712083542574632)
XLA Ops:
  0.0 111.0 %level_solve.1 = f32[8,128,256]{2,1,0:T(8,128)} custom-call(s32[7,1,50]{2,1,0:T(1,128)} %source_hbm.1, s32[7,1,50]{2,1,0:T(1,128)} %target_hbm.1, bf16[8,128,256]{2,1,0:T(8,128)(2,1)} %bitcast.6, bf16[8,128,128]{2,1,0:T(8,128)(2,1)} %bitcast.7, bf16[7,50,128,128]{3,2,1,0:T(8,128)(2,1)} %bitcast.4), custom_call_target="tpu_custom_call" | custom-call | tf_op jit(solution)/shard_map/level_solve/pallas_call | solution.py:308
  111.0 2.3 %copy.7 = f32[1,1,8,128,256]{4,3,2,1,0:T(8,128)} copy(f32[1,1,8,128,256]{4,3,2,1,0:T(8,128)} %bitcast.5) | data formatting | bytes 2097152
